TPU v7x, 32 devices: a whole 2x2x4 slice. The times are simulated.
32 devices in a mesh: gx: 4 (over z), gy: 2 (over y), gz: 4 (over x, core).
Axes of the slice: x: 2, y: 2, z: 4, core: 2. Of those that a mesh axis runs over, the one named last changes fastest.
Arguments:
- populations: float32 [27, 16, 16, 512], P(None, 'gx', 'gy', 'gz'), may hold values from 0.85 to 1.15
- coarse_populations: float32 [27, 32, 8, 256], P(None, 'gx', 'gy', 'gz'), may hold values from 0.85 to 1.15
- fluid_mask: int32 [16, 16, 512], P('gx', 'gy', 'gz'), may hold values 0 or 1
- inflow: float32 [8, 256], P('gy', 'gz'), may hold values from 0.02 to 0.08
- part_dest: int32 [4, 2, 4, 256, 1], P('gx', 'gy', 'gz'), may hold values from 0 to 3; in each aligned block of 256 rows (0 to 255, 256 to 511, ..., all dimensions but the last counted through in order) at most 128 rows name the same one
- part_cell: int32 [4, 2, 4, 256], P('gx', 'gy', 'gz'), may hold values from 0 to 2942, as said below
- part_vel: float32 [4, 2, 4, 3, 256], P('gx', 'gy', 'gz'), may hold values from -0.3 to 0.3
- part_frac: float32 [4, 2, 4, 3, 256], P('gx', 'gy', 'gz'), may hold values from 0 to 1
- part_drag: float32 [4, 2, 4, 256], P('gx', 'gy', 'gz'), may hold values from 0.05 to 0.5
Outputs:
- fine_next: float32 [27, 16, 16, 512], P(None, 'gx', 'gy', 'gz')
- coarse_next: float32 [27, 32, 8, 256], P(None, 'gx', 'gy', 'gz')
Inputs may be any that keep to these rules, and one draw needn't show every extreme that they name: `part_dest`: among the particles of one device at most 128 have the same destination. `part_cell`: ix < 3, iy < 7 and iz < 127, so that all eight corners lie in the destination block.
All inputs are finite; a program needn't handle non-finite values. No bound on the sum of `fluid_mask` on one device may be relied on, other than what follows from the above.
Results may differ from a plain program's by a relative error of at most 0.000078.
Values sent between devices are 32-bit elements; how exact they have to be, the bound alone decides.
A program may use at most 128 MiB of HBM per device.

v0:
```python
import functools

import jax
import jax.numpy as jnp
import numpy as np
from jax import lax
from jax.experimental import pallas as pl
from jax.experimental.pallas import tpu as pltpu
from jax.sharding import PartitionSpec as P

tau_fine = 1.3
tau_coarse = 0.9
stencil_ints = [
    (along_x, along_y, along_z)
    for along_x in (-1, 0, 1)
    for along_y in (-1, 0, 1)
    for along_z in (-1, 0, 1)
]
weights = [
    float(np.float32([8.0 / 27.0, 2.0 / 27.0, 1.0 / 54.0, 1.0 / 216.0][sum(map(abs, c))]))
    for c in stencil_ints
]
prolong_factor = (tau_fine - 1.0) / (2.0 * tau_coarse)
restrict_factor = 2.0 * (tau_coarse - 1.0) / tau_fine
closed = -3.0e38
groups = {
    (dim, side): [i for i, c in enumerate(stencil_ints) if c[dim] == side]
    for dim in range(3)
    for side in (-1, 1)
}
MESH = pl.DeviceIdType.MESH
HIGHEST = lax.Precision.HIGHEST


def moments(get):
    density = None
    sums = [None, None, None]
    for i, c in enumerate(stencil_ints):
        scaled = get(i) * weights[i]
        density = scaled if density is None else density + scaled
        for d in range(3):
            if c[d]:
                if sums[d] is None:
                    sums[d] = -scaled
                else:
                    sums[d] = sums[d] + scaled if c[d] > 0 else sums[d] - scaled
    return density, sums


def equilibria(density, velocity, wanted):
    square = velocity[0] * velocity[0] + velocity[1] * velocity[1] + velocity[2] * velocity[2]
    base = 1.0 - 1.5 * square
    for i in wanted:
        projected = None
        for d in range(3):
            if stencil_ints[i][d]:
                term = velocity[d] if stencil_ints[i][d] > 0 else -velocity[d]
                projected = term if projected is None else projected + term
        if projected is None:
            yield i, density * base
        else:
            yield i, density * (base + 3.0 * projected + 4.5 * projected * projected)


def interface(get, factor, wanted):
    density, sums = moments(get)
    velocity = [s / density for s in sums]
    return [(i, e + factor * (get(i) - e)) for i, e in equilibria(density, velocity, wanted)]


def iota(shape, dim):
    return lax.broadcasted_iota(jnp.int32, shape, dim)


def lane_map(ratio_in, ratio_out):
    rows = iota((128, 128), 0)
    cols = iota((128, 128), 1)
    return (rows // ratio_in == cols // ratio_out).astype(jnp.float32)


def kernel(
    sizes,
    pop,
    coarse,
    mask,
    inflow,
    dest,
    cell,
    vel,
    frac,
    drag,
    fine_out,
    coarse_out,
    parts,
    cbuf,
    cnext,
    fbuf,
    mid,
    force,
    cx_send,
    cx_recv,
    cy_send,
    cy_recv,
    cz_send,
    cz_recv,
    fx_send,
    fx_recv,
    fy_send,
    fy_recv,
    fz_send,
    fz_recv,
    part_sems,
    sems,
):
    n_x, n_y, n_z = sizes
    fx, fy, fz = pop.shape[1:]
    kx, ky, kz = coarse.shape[1:]
    names = ("gx", "gy", "gz")
    counts = (n_x, n_y, n_z)
    where_am_i = [lax.axis_index(a) for a in names]
    me = where_am_i[0]
    is_first = me == 0
    is_last = me == n_x - 1

    for ref in (cy_recv, cz_recv, fy_recv, fz_recv):
        ref[...] = jnp.full(ref.shape, closed, jnp.float32)

    barrier = pltpu.get_barrier_semaphore()
    expected = n_x - 1
    for step in range(1, n_x):
        pl.semaphore_signal(
            barrier, inc=1, device_id={"gx": lax.rem(me + step, n_x)}, device_id_type=MESH
        )
    for d in (1, 2):
        index = where_am_i[d]
        for side in (-1, 1):
            exists = index > 0 if side < 0 else index < counts[d] - 1

            @pl.when(exists)
            def _():
                pl.semaphore_signal(
                    barrier, inc=1, device_id={names[d]: index + side}, device_id_type=MESH
                )

            expected = expected + exists.astype(jnp.int32)

    own = parts.at[me]
    own[0:3, :] = vel[0, 0, 0]
    own[3:6, :] = frac[0, 0, 0]
    own[6:7, :] = drag[0, 0]
    own[7:8, :] = cell[0, 0].astype(jnp.float32)
    own[8:9, :] = dest[...].astype(jnp.float32)
    own[9:16, :] = jnp.zeros((7, dest.shape[1]), jnp.float32)
    pl.semaphore_wait(barrier, expected)

    part_copies = []
    for step in range(1, n_x):
        copy = pltpu.make_async_remote_copy(
            src_ref=own,
            dst_ref=own,
            send_sem=part_sems.at[0, step],
            recv_sem=part_sems.at[1, step],
            device_id={"gx": lax.rem(me + step, n_x)},
            device_id_type=MESH,
        )
        copy.start()
        part_copies.append(copy)

    def neighbour_copy(send, recv, slot, side, number, d):
        index = where_am_i[d]
        if d == 0:
            target = lax.rem(index + side + counts[d], counts[d])
        else:
            target = jnp.clip(index + side, 0, counts[d] - 1)
        return pltpu.make_async_remote_copy(
            src_ref=send.at[slot],
            dst_ref=recv.at[slot],
            send_sem=sems.at[0, number],
            recv_sem=sems.at[1, number],
            device_id={names[d]: target},
            device_id_type=MESH,
        )

    class Exchange:
        def __init__(self, send, recv, d, number):
            self.d = d
            self.copies = [
                neighbour_copy(send, recv, slot, side, number + slot, d)
                for slot, side in ((0, -1), (1, 1))
            ]

        def start(self):
            index, last = where_am_i[self.d], counts[self.d] - 1
            if self.d == 0:
                for copy in self.copies:
                    copy.start()
                return
            pl.when(index > 0)(self.copies[0].start)
            pl.when(index < last)(self.copies[1].start)

        def wait(self):
            index, last = where_am_i[self.d], counts[self.d] - 1
            if self.d == 0:
                for copy in self.copies:
                    copy.wait()
                return

            pl.when(index > 0)(self.copies[0].wait_send)
            pl.when(index < last)(self.copies[0].wait_recv)
            pl.when(index < last)(self.copies[1].wait_send)
            pl.when(index > 0)(self.copies[1].wait_recv)

    def refine(values):
        count = len(values)
        keep = iota((8, 128), 1) < kz
        flat = jnp.concatenate([jnp.where(keep, v, 0.0) for v in values], 0)
        rows = iota((128, 128), 0)
        cols = iota((128, 128), 1)
        spread = (rows == cols // 2).astype(jnp.float32)
        wide = jnp.dot(flat, spread, precision=HIGHEST, preferred_element_type=jnp.float32)
        row = iota((8, 128), 0)
        out = []
        for k in range(count):
            tile = wide[8 * k : 8 * k + 8]
            made = tile
            for by in range(1, 5):
                moved = pltpu.roll(tile, by, 0)
                made = jnp.where((row + 1) // 2 == by, moved, made)
            out.append(made)
        return out

    def late(get, send, number):
        made = interface(get, prolong_factor, groups[0, 1])
        return refine([v for _, v in made])

    cnext[...] = jnp.ones(cnext.shape, jnp.float32)
    for i in range(27):
        cnext[i, :, 0:ky, 0:kz] = coarse[i]

    density, sums = moments(lambda i: cnext[i])
    velocity = [s / density for s in sums]
    for i, e in equilibria(density, velocity, range(27)):
        n = cnext[i]
        cbuf[i] = n - (n - e) * (1.0 / tau_coarse)

    ahead = [pop[i, 0] + pop[i, 1] for i in range(27)]
    flat = jnp.concatenate(ahead, 0)
    gather_lanes = (iota((128, 128), 0) // 2 == iota((128, 128), 1)).astype(jnp.float32)
    narrow = jnp.dot(flat, gather_lanes, precision=HIGHEST, preferred_element_type=jnp.float32)
    row = iota((8, 128), 0)
    means = []
    for i in range(27):
        tile = narrow[8 * i : 8 * i + 8]
        tile = tile + pltpu.roll(tile, 7, 0)
        made = tile
        for by in range(1, 4):
            made = jnp.where(row == by, pltpu.roll(tile, 8 - by, 0), made)
        means.append(0.125 * made)
    restricted = interface(lambda i: means[i], restrict_factor, groups[0, -1])
    for k, (i, v) in enumerate(restricted):
        cx_send[0, k] = jnp.where(is_first, v, cbuf[i, 0])
    for k, i in enumerate(groups[0, 1]):
        cx_send[1, k] = cbuf[i, kx - 1]
    exchange_cx = Exchange(cx_send, cx_recv, 0, 0)
    exchange_cx.start()

    start_ghost = late(lambda i: cnext[i, kx - 1], None, 0)

    fluid = mask[...].astype(jnp.float32)
    open_cells = mask[...] > 0
    density, sums = moments(lambda i: pop[i])
    safe = density + (1.0 - fluid)
    inverse = 1.0 / safe
    cell_velocity = [s * inverse for s in sums]
    sample_from = jnp.concatenate(
        [v.reshape(fx * fy, fz).T for v in cell_velocity], 0
    )
    for copy in part_copies:
        copy.wait()
    total = None
    for source in range(n_x):
        block = parts[source]
        width = block.shape[1]
        where_cell = block[7:8].astype(jnp.int32)
        mine = block[8:9].astype(jnp.int32) == me
        first_row = jnp.where(mine, where_cell // fz, -1000)
        first_lane = where_cell % fz
        f_x, f_y, f_z = block[3:4], block[4:5], block[5:6]
        offset = iota((fx * fy, width), 0) - first_row
        across = (
            jnp.where(offset == 0, (1.0 - f_x) * (1.0 - f_y), 0.0)
            + jnp.where(offset == 1, (1.0 - f_x) * f_y, 0.0)
            + jnp.where(offset == fy, f_x * (1.0 - f_y), 0.0)
            + jnp.where(offset == fy + 1, f_x * f_y, 0.0)
        )
        offset = iota((fz, width), 0) - first_lane
        along = jnp.where(offset == 0, 1.0 - f_z, 0.0) + jnp.where(offset == 1, f_z, 0.0)
        lines = jnp.dot(
            sample_from, across, precision=HIGHEST, preferred_element_type=jnp.float32
        )
        pushes = []
        for d in range(3):
            sampled = jnp.sum(lines[d * fz : (d + 1) * fz] * along, axis=0, keepdims=True)
            impulse = block[6:7] * (block[d : d + 1] - sampled)
            pushes.append(along * impulse)
        added = lax.dot_general(
            across,
            jnp.concatenate(pushes, 0),
            (((1,), (1,)), ((), ())),
            precision=HIGHEST,
            preferred_element_type=jnp.float32,
        )
        total = added if total is None else total + added
    for d in range(3):
        force[d] = total[:, d * fz : (d + 1) * fz].reshape(fx, fy, fz)

    def fine_collide(get, density, sums, ghost, exchange, slot):
        safe = density + (1.0 - fluid)
        inverse = 1.0 / safe
        velocity = [(sums[d] + tau_fine * force[d]) * inverse for d in range(3)]
        for i, e in equilibria(safe, velocity, range(27)):
            n = get(i)
            fbuf[i] = jnp.where(open_cells, n - (n - e) * (1.0 / tau_fine), closed)
        for k, i in enumerate(groups[0, 1]):
            fx_send[slot, 1, k] = jnp.where(is_last, ghost[k], fbuf[i, fx - 1])
        for k, i in enumerate(groups[0, -1]):
            fx_send[slot, 0, k] = fbuf[i, 0]
        exchange.start()

    def shift_x(post, recv, stage, low, high, last):
        for i, c in enumerate(stencil_ints):
            if c[0] == 0:
                stage[i] = post[i]
            elif c[0] > 0:
                stage[i, 0] = low(i)
                for x in range(1, last + 1):
                    stage[i, x] = post[i, x - 1]
            else:
                stage[i, last] = high(i)
                for x in range(last):
                    stage[i, x] = post[i, x + 1]

    def send_y(stage, send, edge, exchange):
        for k, i in enumerate(groups[1, 1]):
            send[1, k] = stage[i, :, edge, :]
        for k, i in enumerate(groups[1, -1]):
            send[0, k] = stage[i, :, 0, :]
        exchange.start()

    def shift_y(stage, recv, edge, exchange):
        exchange.wait()
        row = iota(stage.shape[1:], 1)
        for side, slot, at, by in ((1, 1, 0, 1), (-1, 0, edge, 7)):
            for k, i in enumerate(groups[1, side]):
                stage[i] = jnp.where(
                    row == at, recv[slot, k][:, None, :], pltpu.roll(stage[i], by, 1)
                )

    def send_z(stage, send, edge, exchange):
        lane = iota(stage.shape[1:], 2)
        for side, slot, at in ((1, 1, edge), (-1, 0, 0)):
            packed = jnp.zeros(stage.shape[1:], jnp.float32)
            for k, i in enumerate(groups[2, side]):
                moved = pltpu.roll(stage[i], (k - at) % 128, 2)
                packed = jnp.where(lane == k, moved, packed)
            send[slot] = packed
        exchange.start()

    def shift_z(stage, recv, edge, exchange):
        exchange.wait()
        lane = iota(stage.shape[1:], 2)

        def get(i):
            side = stencil_ints[i][2]
            if side == 0:
                return stage[i]
            slot, at, by = (1, 0, 1) if side > 0 else (0, edge, 127)
            k = groups[2, side].index(i)
            column = pltpu.roll(recv[slot], (at - k) % 128, 2)
            return jnp.where(lane == at, column, pltpu.roll(stage[i], by, 2))

        return get

    fine_x = [Exchange(fx_send.at[s], fx_recv.at[s], 0, 6 + 6 * s) for s in (0, 1)]
    fine_y = [Exchange(fy_send.at[s], fy_recv.at[s], 1, 8 + 6 * s) for s in (0, 1)]
    fine_z = [Exchange(fz_send.at[s], fz_recv.at[s], 2, 10 + 6 * s) for s in (0, 1)]
    coarse_y = Exchange(cy_send, cy_recv, 1, 2)
    coarse_z = Exchange(cz_send, cz_recv, 2, 4)

    fine_collide(lambda i: pop[i], density, sums, start_ghost, fine_x[0], 0)

    exchange_cx.wait()
    speed = jnp.ones((8, 128), jnp.float32)
    cx_recv_low = {}
    zero = jnp.zeros((8, 128), jnp.float32)
    speed = inflow[...]
    for i, e in equilibria(1.0, [speed, zero, zero], groups[0, 1]):
        cx_recv_low[i] = jnp.where(is_first, e, cx_recv[1, groups[0, 1].index(i)])
    shift_x(
        cbuf, cx_recv, cnext, lambda i: cx_recv_low[i], lambda i: cx_recv[0, i], kx - 1
    )
    send_y(cnext, cy_send, ky - 1, coarse_y)

    def fine_x_phase(s):
        fine_x[s].wait()
        shift_x(
            fbuf,
            fx_recv,
            mid,
            lambda i: fx_recv[s, 1, i - 18],
            lambda i: jnp.where(is_last, fbuf[i, fx - 1], fx_recv[s, 0, i]),
            fx - 1,
        )
        send_y(mid, fy_send.at[s], fy - 1, fine_y[s])

    def finish_fine(s, out):
        get = shift_z(mid, fz_recv.at[s], fz - 1, fine_z[s])
        for i in range(27):
            v = get(i)
            v = jnp.where(v == closed, fbuf[26 - i], v)
            out[i] = jnp.where(open_cells, v, 0.0)

    fine_x_phase(0)
    shift_y(cnext, cy_recv, ky - 1, coarse_y)
    send_z(cnext, cz_send, kz - 1, coarse_z)
    shift_y(mid, fy_recv.at[0], fy - 1, fine_y[0])
    send_z(mid, fz_send.at[0], fz - 1, fine_z[0])

    get = shift_z(cnext, cz_recv, kz - 1, coarse_z)
    for i in range(27):
        v = get(i)
        v = jnp.where(v == closed, cbuf[26 - i], v)
        coarse_out[i] = v[:, 0:ky, 0:kz]
        cnext[i] = v
    half = jnp.ones((8, 128), jnp.float32)

    def halfway(i):
        layer = cnext[i, kx - 1, 0:ky, 0:kz]
        return 0.5 * (coarse[i, kx - 1] + layer)

    made = interface(halfway, prolong_factor, groups[0, 1])
    for k, (i, v) in enumerate(made):
        cx_send[0, k, 0:ky, 0:kz] = v
    late_ghost = refine([cx_send[0, k] for k in range(9)])

    finish_fine(0, fine_out)
    density, sums = moments(lambda i: fine_out[i])
    fine_collide(lambda i: fine_out[i], density, sums, late_ghost, fine_x[1], 1)
    fine_x_phase(1)
    shift_y(mid, fy_recv.at[1], fy - 1, fine_y[1])
    send_z(mid, fz_send.at[1], fz - 1, fine_z[1])
    finish_fine(1, fine_out)


def body(sizes, populations, coarse, mask, inflow, dest, cell, vel, frac, drag):
    fx, fy, fz = populations.shape[1:]
    kx, ky, kz = coarse.shape[1:]
    n_x = sizes[0]
    width = drag.shape[-1]
    padded = jnp.pad(inflow, ((0, 8 - ky), (0, 128 - kz)))
    vmem = pl.BlockSpec(memory_space=pltpu.VMEM)
    f32 = jnp.float32
    return pl.pallas_call(
        functools.partial(kernel, sizes),
        out_shape=(
            jax.ShapeDtypeStruct(populations.shape, f32),
            jax.ShapeDtypeStruct(coarse.shape, f32),
        ),
        in_specs=[vmem] * 9,
        out_specs=(vmem, vmem),
        scratch_shapes=[
            pltpu.VMEM((n_x, 16, width), f32),
            pltpu.VMEM((27, kx, 8, 128), f32),
            pltpu.VMEM((27, kx, 8, 128), f32),
            pltpu.VMEM((27, fx, fy, fz), f32),
            pltpu.VMEM((27, fx, fy, fz), f32),
            pltpu.VMEM((3, fx, fy, fz), f32),
            pltpu.VMEM((2, 9, 8, 128), f32),
            pltpu.VMEM((2, 9, 8, 128), f32),
            pltpu.VMEM((2, 9, kx, 128), f32),
            pltpu.VMEM((2, 9, kx, 128), f32),
            pltpu.VMEM((2, kx, 8, 128), f32),
            pltpu.VMEM((2, kx, 8, 128), f32),
            pltpu.VMEM((2, 2, 9, fy, fz), f32),
            pltpu.VMEM((2, 2, 9, fy, fz), f32),
            pltpu.VMEM((2, 2, 9, fx, fz), f32),
            pltpu.VMEM((2, 2, 9, fx, fz), f32),
            pltpu.VMEM((2, 2, fx, fy, fz), f32),
            pltpu.VMEM((2, 2, fx, fy, fz), f32),
            pltpu.SemaphoreType.DMA((2, n_x)),
            pltpu.SemaphoreType.DMA((2, 18)),
        ],
        compiler_params=pltpu.CompilerParams(collective_id=0, has_side_effects=True),
    )(populations, coarse, mask, padded, dest.reshape(1, width), cell, vel, frac, drag)


def solution(mesh):
    sizes = tuple(mesh.shape[a] for a in ("gx", "gy", "gz"))
    return jax.shard_map(
        functools.partial(body, sizes),
        mesh=mesh,
        in_specs=(
            P(None, "gx", "gy", "gz"),
            P(None, "gx", "gy", "gz"),
            P("gx", "gy", "gz"),
            P("gy", "gz"),
            P("gx", "gy", "gz", None, None),
            P("gx", "gy", "gz", None),
            P("gx", "gy", "gz", None, None),
            P("gx", "gy", "gz", None, None),
            P("gx", "gy", "gz", None),
        ),
        out_specs=(P(None, "gx", "gy", "gz"), P(None, "gx", "gy", "gz")),
        check_vma=False,
    )
```

profile of v0, /device:TPU:1, one launch (start us, length us, event | category | flops | bytes accessed | tf_op | source)
XLA Modules:
  0.0 39.1 jit_solution(10040528532263851481)
XLA Ops:
  0.6 0.0 copy-start.1
  0.6 1.3 %pad.4.inflow = f32[8,128]{1,0:T(8,128)} pad(f32[4,64]{1,0:T(4,128)} %param.12, f32[]{:T(128)} %constant.2.clone.1), padding=0_4x0_64 | pad | bytes 5124 | tf_op jit(solution)/shard_map/jit(_pad)/pad | solution.py:460
  1.9 0.0 copy-done.1
  1.9 0.0 copy-start.2
  1.9 0.6 %copy.11.vel = f32[1,1,1,3,256]{4,3,2,1,0:T(4,128)} copy(f32[1,1,1,3,256]{4,2,3,1,0:T(1,128)S(1)} %copy-done.1) | data formatting | bytes 6144 | tf_op args[6]
  2.5 0.1 copy-done.2
  2.6 0.6 %copy.12.frac = f32[1,1,1,3,256]{4,3,2,1,0:T(4,128)} copy(f32[1,1,1,3,256]{4,2,3,1,0:T(1,128)S(1)} %copy-done.2) | data formatting | bytes 6144 | tf_op args[7]
  3.2 33.2 %shard_map.104 = (f32[27,4,8,128]{3,2,1,0:T(8,128)}, f32[27,8,4,64]{3,2,1,0:T(4,128)}) custom-call(f32[27,4,8,128]{3,2,1,0:T(8,128)} %pop.1, f32[27,8,4,64]{3,2,1,0:T(4,128)} %coarse.1, s32[4,8,128]{2,1,0:T(8,128)} %mask.1, f32[8,128]{1,0:T(8,128)} %pad.4.inflow, s32[1,256]{1,0:T(1,128)} %bitcast.1, s32[1,1,1,256]{3,2,1,0:T(1,128)} %cell.1, ...), custom_call_target="tpu_custom_call" | custom-call | tf_op jit(solution)/shard_map/pallas_call | solution.py:463
  36.4 0.0 copy-start
  36.4 1.9 %copy.15 = f32[27,4,8,128]{3,2,1,0:T(8,128)} copy(f32[27,4,8,128]{3,2,1,0:T(8,128)} %get-tuple-element.4) | data formatting | bytes 884736
  38.3 0.0 copy-done
  38.3 0.8 %copy.16 = f32[27,8,4,64]{3,2,1,0:T(4,128)} copy(f32[27,8,4,64]{3,2,1,0:T(4,128)S(1)} %copy-done) | data formatting | bytes 442368
Async XLA Ops:
  0.6 1.3 %copy-start.1 = (f32[1,1,1,3,256]{4,2,3,1,0:T(1,128)S(1)}, f32[1,1,1,3,256]{4,2,3,1,0:T(1,128)}, u32[]{:S(2)}) copy-start(f32[1,1,1,3,256]{4,2,3,1,0:T(1,128)} %param.15) | copy-start | bytes 9220
  1.9 0.7 %copy-start.2 = (f32[1,1,1,3,256]{4,2,3,1,0:T(1,128)S(1)}, f32[1,1,1,3,256]{4,2,3,1,0:T(1,128)}, u32[]{:S(2)}) copy-start(f32[1,1,1,3,256]{4,2,3,1,0:T(1,128)} %param.16) | copy-start | bytes 9220
  36.4 1.9 %copy-start = (f32[27,8,4,64]{3,2,1,0:T(4,128)S(1)}, f32[27,8,4,64]{3,2,1,0:T(4,128)}, u32[]{:S(2)}) copy-start(f32[27,8,4,64]{3,2,1,0:T(4,128)} %get-tuple-element.5) | copy-start | bytes 663556
where the time goes:
time: 39.3 us; the launch traced here: 39.1 us
  Pallas kernels  33.2 us (84%)
  local copies, waits for them, and re-layouts  5.19 us (13%)
  between operations  0.66 us (2%)
    pallas_call x1, Pallas kernels, body(): pl.pallas_call(functools.partial(kernel, sizes), out_shape=(jax.ShapeDtyp...  33.2 us
    unnamed x10, local copies, waits for them, and re-layouts  3.91 us
    pad x1, local copies, waits for them, and re-layouts, body(): padded = jnp.pad(inflow, ((0, 8 - ky), (0, 128 - kz)))  1.28 us

commit v1 on v0

--- a/solution.py
+++ b/solution.py
@@ -97,6 +97,7 @@
     fbuf,
     mid,
     force,
+    inlet,
     cx_send,
     cx_recv,
     cy_send,
@@ -145,8 +146,9 @@
             expected = expected + exists.astype(jnp.int32)
 
     own = parts.at[me]
-    own[0:3, :] = vel[0, 0, 0]
-    own[3:6, :] = frac[0, 0, 0]
+    for d in range(3):
+        own[d : d + 1, :] = vel[d]
+        own[3 + d : 4 + d, :] = frac[d]
     own[6:7, :] = drag[0, 0]
     own[7:8, :] = cell[0, 0].astype(jnp.float32)
     own[8:9, :] = dest[...].astype(jnp.float32)
@@ -278,8 +280,8 @@
     for copy in part_copies:
         copy.wait()
     total = None
-    for source in range(n_x):
-        block = parts[source]
+    for first in range(0, n_x, 4):
+        block = jnp.concatenate([parts[s] for s in range(first, min(first + 4, n_x))], 1)
         width = block.shape[1]
         where_cell = block[7:8].astype(jnp.int32)
         mine = block[8:9].astype(jnp.int32) == me
@@ -390,10 +392,11 @@
     fine_collide(lambda i: pop[i], density, sums, start_ghost, fine_x[0], 0)
 
     exchange_cx.wait()
-    speed = jnp.ones((8, 128), jnp.float32)
     cx_recv_low = {}
     zero = jnp.zeros((8, 128), jnp.float32)
-    speed = inflow[...]
+    inlet[...] = zero
+    inlet[0:ky, 0:kz] = inflow[...]
+    speed = inlet[...]
     for i, e in equilibria(1.0, [speed, zero, zero], groups[0, 1]):
         cx_recv_low[i] = jnp.where(is_first, e, cx_recv[1, groups[0, 1].index(i)])
     shift_x(
@@ -432,7 +435,6 @@
         v = jnp.where(v == closed, cbuf[26 - i], v)
         coarse_out[i] = v[:, 0:ky, 0:kz]
         cnext[i] = v
-    half = jnp.ones((8, 128), jnp.float32)
 
     def halfway(i):
         layer = cnext[i, kx - 1, 0:ky, 0:kz]
@@ -457,7 +459,6 @@
     kx, ky, kz = coarse.shape[1:]
     n_x = sizes[0]
     width = drag.shape[-1]
-    padded = jnp.pad(inflow, ((0, 8 - ky), (0, 128 - kz)))
     vmem = pl.BlockSpec(memory_space=pltpu.VMEM)
     f32 = jnp.float32
     return pl.pallas_call(
@@ -475,6 +476,7 @@
             pltpu.VMEM((27, fx, fy, fz), f32),
             pltpu.VMEM((27, fx, fy, fz), f32),
             pltpu.VMEM((3, fx, fy, fz), f32),
+            pltpu.VMEM((8, 128), f32),
             pltpu.VMEM((2, 9, 8, 128), f32),
             pltpu.VMEM((2, 9, 8, 128), f32),
             pltpu.VMEM((2, 9, kx, 128), f32),
@@ -491,7 +493,7 @@
             pltpu.SemaphoreType.DMA((2, 18)),
         ],
         compiler_params=pltpu.CompilerParams(collective_id=0, has_side_effects=True),
-    )(populations, coarse, mask, padded, dest.reshape(1, width), cell, vel, frac, drag)
+    )(populations, coarse, mask, inflow, dest.reshape(1, width), cell, vel.reshape(3, 1, width), frac.reshape(3, 1, width), drag)
 
 
 def solution(mesh):

time: 39.3 us -> 35.9 us (0.913)
  local copies, waits for them, and re-layouts: 5.19 us -> 2.62 us
  Pallas kernels: 33.2 us -> 32.5 us
    pad x1 -> x0, local copies, waits for them, and re-layouts: 1.28 us -> none  [body(): padded = jnp.pad(inflow, ((0, 8 - ky), (0, 128 - kz)))]
    unnamed x10 -> x4, local copies, waits for them, and re-layouts: 3.91 us -> 2.62 us
    pallas_call x1, Pallas kernels: 33.2 us -> 32.5 us  [body(): pl.pallas_call(functools.partial(kernel, sizes), out_shape=(jax.ShapeDtyp...]
where the time goes in v1:
time: 35.9 us; the launch traced here: 35.8 us
  Pallas kernels  32.5 us (91%)
  local copies, waits for them, and re-layouts  2.62 us (7%)
  between operations  0.65 us (2%)
    pallas_call x1, Pallas kernels, body(): pl.pallas_call(functools.partial(kernel, sizes), out_shape=(jax.ShapeDtyp...  32.5 us
    unnamed x4, local copies, waits for them, and re-layouts  2.62 us

profile of v1, /device:TPU:1, one launch (start us, length us, event | category | flops | bytes accessed | tf_op | source)
XLA Modules:
  0.0 35.8 jit_solution(2138648413423353016)
XLA Ops:
  0.6 32.5 %shard_map.104 = (f32[27,4,8,128]{3,2,1,0:T(8,128)}, f32[27,8,4,64]{3,2,1,0:T(4,128)}) custom-call(f32[27,4,8,128]{3,2,1,0:T(8,128)} %pop.1, f32[27,8,4,64]{3,2,1,0:T(4,128)} %coarse.1, s32[4,8,128]{2,1,0:T(8,128)} %mask.1, f32[4,64]{1,0:T(4,128)} %inflow.1, s32[1,256]{1,0:T(1,128)} %bitcast.5, s32[1,1,1,256]{3,2,1,0:T(1,128)} %cell.1, ...), custom_call_target="tpu_custom_call" | custom-call | tf_op jit(solution)/shard_map/pallas_call | solution.py:464
  33.2 0.0 copy-start
  33.2 1.9 %copy.13 = f32[27,4,8,128]{3,2,1,0:T(8,128)} copy(f32[27,4,8,128]{3,2,1,0:T(8,128)} %get-tuple-element.4) | data formatting | bytes 884736
  35.0 0.0 copy-done
  35.0 0.8 %copy.14 = f32[27,8,4,64]{3,2,1,0:T(4,128)} copy(f32[27,8,4,64]{3,2,1,0:T(4,128)S(1)} %copy-done) | data formatting | bytes 442368
Async XLA Ops:
  33.2 1.9 %copy-start = (f32[27,8,4,64]{3,2,1,0:T(4,128)S(1)}, f32[27,8,4,64]{3,2,1,0:T(4,128)}, u32[]{:S(2)}) copy-start(f32[27,8,4,64]{3,2,1,0:T(4,128)} %get-tuple-element.5) | copy-start | bytes 663556
